TPU v7x, 32 devices: a whole 2x2x4 slice. The times are simulated.
32 devices in a mesh: gx: 2 (over core), gy: 4 (over y, x), ma: 4 (over z).
Axes of the slice: x: 2, y: 2, z: 4, core: 2. Of those that a mesh axis runs over, the one named last changes fastest.
Arguments:
- object_field: float32 [2, 256, 1024], P(None, 'gx', 'gy'), may hold values from -5 to 5
- probe_modes: float32 [8, 2, 256, 256], P('ma'), may hold values from -1.5 to 1.5
- measured: float32 [2, 4, 2, 256, 256], P('gx', 'gy'), may hold values from 0.1 to 4
- positions: int32 [2, 4, 2, 2], P('gx', 'gy'), may hold values from 0 to 255, as said below
- slot_counts: int32 [2, 4], P('gx', 'gy'), may hold values from 1 to 2, as said below
Outputs:
- updated_object: float32 [2, 256, 1024], P(None, 'gx', 'gy')
Inputs may be any that keep to these rules, and one draw needn't show every extreme that they name: positions[a, b, s] holds a row 0 to 127 and a column 0 to 255 of tile (a, b); slots s >= slot_counts[a, b] are unused. `slot_counts`: some tile uses all 2 slots.
All inputs are finite; a program needn't handle non-finite values.
Results may differ from a plain program's by a relative error of at most 0.0023.
Values sent between devices are 32-bit elements; how exact they have to be, the bound alone decides.
A program may use at most 64 MiB of HBM per device.

v0:
```python
import math
import jax
import jax.numpy as jnp
from jax import lax
from jax.sharding import PartitionSpec as P

OUTER = 2
DAMPING = 1.0


def padded_2(block, sides, width):
    for axis, dim in sides:
        count = lax.axis_size(axis)
        forward = [(i, i + 1) for i in range(count - 1)]
        backward = [(target, source) for source, target in forward]
        low = lax.ppermute(
            lax.slice_in_dim(block, block.shape[dim] - width, None, axis=dim), axis, forward
        )
        high = lax.ppermute(lax.slice_in_dim(block, 0, width, axis=dim), axis, backward)
        block = jnp.concatenate([low, block, high], axis=dim)
    return block


def dft_tables(patch_width):
    ladder = jnp.arange(patch_width, dtype=jnp.int32)
    phases = ladder[:, None] * ladder[None, :] % patch_width
    angles = phases.astype(jnp.float32) * (2.0 * math.pi / patch_width)
    factor = 1.0 / math.sqrt(patch_width)
    real_part = jnp.cos(angles) * factor
    imag_part = -jnp.sin(angles) * factor
    table_one = jnp.concatenate(
        [jnp.concatenate([real_part, -imag_part], 1), jnp.concatenate([imag_part, real_part], 1)], 0
    ).astype(jnp.bfloat16)
    table_two = jnp.concatenate(
        [jnp.concatenate([real_part, imag_part], 1), jnp.concatenate([-imag_part, real_part], 1)], 0
    ).astype(jnp.bfloat16)
    return (table_one, table_two)


def forward_transform(wavefield, tables):
    patch_width = wavefield.shape[-1]
    halfway = jnp.einsum(
        "pqci,bcik->bpqk",
        tables[0].reshape(2, patch_width, 2, patch_width),
        wavefield,
        preferred_element_type=jnp.float32,
    ).astype(jnp.bfloat16)
    return jnp.einsum(
        "bcik,ckl->bil",
        halfway,
        tables[1].reshape(2, patch_width, 2 * patch_width),
        preferred_element_type=jnp.float32,
    )


def adjoint_transform(weighted, tables):
    patch_width = weighted.shape[1]
    halfway = jnp.einsum(
        "bik,kl->bil", weighted, tables[0], preferred_element_type=jnp.float32
    ).astype(jnp.bfloat16)
    return jnp.einsum(
        "pqci,bicl->bpql",
        tables[1].reshape(2, patch_width, 2, patch_width),
        halfway.reshape(halfway.shape[0], patch_width, 2, patch_width),
        preferred_element_type=jnp.float32,
    )


def exit_waves(probe_modes, windows):
    probe_real = probe_modes[None, :, 0]
    probe_imag = probe_modes[None, :, 1]
    window_real = windows[:, None, 0]
    window_imag = windows[:, None, 1]
    real_part = probe_real * window_real - probe_imag * window_imag
    imag_part = probe_real * window_imag + probe_imag * window_real
    wavefield = jnp.stack([real_part, imag_part], 2).astype(jnp.bfloat16)
    return wavefield.reshape(-1, 2, probe_modes.shape[-1], probe_modes.shape[-1])


def intensity_part(spectra, mode_count):
    patch_width = spectra.shape[1]
    grouped = spectra.reshape(-1, mode_count, patch_width, 2 * patch_width)
    squared = grouped * grouped
    return jnp.sum(squared[..., :patch_width] + squared[..., patch_width:], axis=1)


def change_part(spectra, moved_spectra, mode_count):
    patch_width = spectra.shape[1]
    grouped = spectra.reshape(-1, mode_count, patch_width, 2 * patch_width)
    shifted = moved_spectra.reshape(-1, mode_count, patch_width, 2 * patch_width)
    product = grouped * shifted
    return 2.0 * jnp.sum(product[..., :patch_width] + product[..., patch_width:], axis=1)


def mode_images(weights, spectra, probe_modes, tables):
    mode_count = probe_modes.shape[0]
    patch_width = probe_modes.shape[-1]
    doubled = jnp.concatenate([weights, weights], -1)
    grouped = spectra.reshape(-1, mode_count, patch_width, 2 * patch_width)
    weighted = (2.0 * grouped * doubled[:, None]).astype(jnp.bfloat16)
    returned = adjoint_transform(weighted.reshape(-1, patch_width, 2 * patch_width), tables)
    returned = returned.reshape(-1, mode_count, 2, patch_width, patch_width)
    probe_real = probe_modes[None, :, 0]
    probe_imag = probe_modes[None, :, 1]
    real_part = jnp.sum(probe_real * returned[:, :, 0] + probe_imag * returned[:, :, 1], axis=1)
    imag_part = jnp.sum(probe_real * returned[:, :, 1] - probe_imag * returned[:, :, 0], axis=1)
    return jnp.stack([real_part, imag_part], 1)


def fold_edges(widened, axis_dim, length, rim_width):
    middle = lax.slice_in_dim(widened, 2 * rim_width, 2 * rim_width + length, axis=axis_dim)
    low_rim = lax.slice_in_dim(widened, 0, rim_width, axis=axis_dim)
    high_rim = lax.slice_in_dim(
        widened, length + 3 * rim_width, length + 4 * rim_width, axis=axis_dim
    )
    low_pads = [(0, 0), (0, 0), (0, 0)]
    high_pads = [(0, 0), (0, 0), (0, 0)]
    low_pads[axis_dim] = (0, length - rim_width)
    high_pads[axis_dim] = (length - rim_width, 0)
    return middle + jnp.pad(low_rim, low_pads) + jnp.pad(high_rim, high_pads)


def shards(object_field, probe_modes, measured, positions, slot_counts):
    patch_width = probe_modes.shape[-1]
    mode_count = probe_modes.shape[0]
    rim_width = patch_width // 2
    tile_rows = object_field.shape[1]
    tile_cols = object_field.shape[2]
    slot_count = measured.shape[2]
    share_rows = tile_rows // lax.axis_size("ma")
    tables = dft_tables(patch_width)
    targets = measured[0, 0]
    centres = positions[0, 0]
    live_mask = (jnp.arange(slot_count, dtype=jnp.int32) < slot_counts[0, 0]).astype(jnp.float32)[
        :, None, None
    ]
    anchor = jnp.zeros((), jnp.int32)

    def spectra_of(current):
        padded = padded_2(current, (("gx", 1), ("gy", 2)), rim_width)
        windows = jnp.stack(
            [
                lax.dynamic_slice(
                    padded,
                    (anchor, centres[slot_index, 0], centres[slot_index, 1]),
                    (2, patch_width, patch_width),
                )
                for slot_index in range(slot_count)
            ],
            0,
        )
        return forward_transform(exit_waves(probe_modes, windows), tables)

    def mode_total(partial_value):
        return lax.psum(partial_value, "ma")

    def combine(folded):
        summed = lax.psum(folded, "ma")
        return summed

    def project(weights, spectra):
        pieces = mode_images(weights, spectra, probe_modes, tables)
        extended = jnp.zeros((2, tile_rows + patch_width, tile_cols + patch_width), jnp.float32)
        for slot_index in range(slot_count):
            corner = (anchor, centres[slot_index, 0], centres[slot_index, 1])
            extended = lax.dynamic_update_slice(
                extended,
                lax.dynamic_slice(extended, corner, (2, patch_width, patch_width))
                + pieces[slot_index],
                corner,
            )
        widened = padded_2(extended, (("gx", 1), ("gy", 2)), rim_width)
        folded = fold_edges(fold_edges(widened, 1, tile_rows, rim_width), 2, tile_cols, rim_width)
        result = combine(folded)
        return result

    def local_sum(first_vec, second_vec):
        first_vec = lax.dynamic_slice_in_dim(
            first_vec, lax.axis_index("ma") * share_rows, share_rows, 1
        )
        second_vec = lax.dynamic_slice_in_dim(
            second_vec, lax.axis_index("ma") * share_rows, share_rows, 1
        )
        return jnp.sum(first_vec * second_vec)

    current = object_field
    for outer_step in range(OUTER):
        spectra = spectra_of(current)
        misfit = live_mask * (mode_total(intensity_part(spectra, mode_count)) - targets)
        gradient = project(misfit, spectra)
        residual = -gradient
        direction = residual
        norm_now = lax.psum(local_sum(residual, residual), ("gx", "gy", "ma"))
        moved_spectra = spectra_of(direction)
        change = live_mask * mode_total(change_part(spectra, moved_spectra, mode_count))
        applied = project(change, spectra) + DAMPING * direction
        step_size = norm_now / lax.psum(local_sum(direction, applied), ("gx", "gy", "ma"))
        update = step_size * direction
        residual = residual - step_size * applied
        current = current + update
    return current


def solution(mesh):
    return jax.shard_map(
        shards,
        mesh=mesh,
        in_specs=(
            P(None, "gx", "gy"),
            P("ma", None, None, None),
            P("gx", "gy", None, None, None),
            P("gx", "gy", None, None),
            P("gx", "gy"),
        ),
        out_specs=P(None, "gx", "gy"),
        check_vma=False,
    )
```

profile of v0, /device:TPU:0, one launch (start us, length us, event | category | flops | bytes accessed | tf_op | source)
XLA Modules:
  0.0 797.4 jit_solution(15070351154825093424)
XLA Ops:
  6.5 2.5 collective-permute-start
  13.7 4.2 collective-permute-start.2
  31.0 6.3 collective-permute-done.3
  42.5 2.0 convert_element_type.140
  45.2 36.4 %all-reduce.15.cloned.1.call-done = f32[2,256,256]{2,1,0:T(8,128)} async-done(((f32[2,256,256]{2,1,0:T(8,128)}), f32[2,256,256]{2,1,0:T(8,128)}) %all-reduce.15.cloned.1.call-update) | async-done | bytes 524304 | tf_op jit(solution)/shard_map/psum | solution.py:155
  84.1 1.7 convolution_convert_fusion.3
  85.8 1.5 copy.167
  89.5 7.8 dynamic_update_slice.24
  97.3 2.0 fusion.50
  99.3 8.2 %dynamic_update_slice.25 = f32[2,384,512]{1,2,0:T(8,128)S(1)} dynamic-update-slice(f32[2,384,512]{1,2,0:T(8,128)S(1)} %dynamic_update_slice.24, f32[2,256,256]{1,2,0:T(8,128)} %fusion.50, s32[]{:T(128)} %constant.15.clone.1, s32[]{:T(128)S(6)} %select_n.33, s32[]{:T(128)S(6)} %select_n.34) | dynamic-update-slice | bytes 1048580 | tf_op jit(solution)/shard_map/dynamic_update_slice | solution.py:166
  110.4 2.3 collective-permute-done.5
  112.8 3.3 collective-permute-start.6
  117.4 12.9 %collective-permute-done.6 = f32[2,640,128]{1,2,0:T(8,128)S(1)} collective-permute-done((f32[2,640,128]{1,2,0:T(8,128)S(1)}, f32[2,640,128]{1,2,0:T(8,128)S(1)}, u32[]{:S(2)}, u32[]{:S(2)}) %collective-permute-start.6) | collective-permute-done | bytes 655392 | tf_op jit(solution)/shard_map/ppermute | solution.py:16
  130.4 16.7 %collective-permute-done.7 = f32[2,640,128]{1,2,0:T(8,128)S(1)} collective-permute-done((f32[2,640,128]{1,2,0:T(8,128)S(1)}, f32[2,640,128]{1,2,0:T(8,128)S(1)}, u32[]{:S(2)}, u32[]{:S(2)}) %collective-permute-start.7) | collective-permute-done | bytes 655392 | tf_op jit(solution)/shard_map/ppermute | solution.py:19
  148.6 33.7 %all-reduce.17.cloned.1.call-done = f32[2,128,256]{1,2,0:T(8,128)} async-done(((f32[2,128,256]{1,2,0:T(8,128)}), f32[2,128,256]{1,2,0:T(8,128)}) %all-reduce.17.cloned.1.call-update) | async-done | bytes 262160 | tf_op jit(solution)/shard_map/psum | solution.py:158
  185.9 2.1 collective-permute-done.9
  188.2 3.4 collective-permute-start.10
  191.6 1.5 collective-permute-start.11
  193.0 7.2 collective-permute-done.10
  200.2 10.3 %collective-permute-done.11 = f32[2,384,128]{1,2,0:T(8,128)S(1)} collective-permute-done((f32[2,384,128]{1,2,0:T(8,128)S(1)}, f32[2,384,128]{1,2,0:T(8,128)S(1)}, u32[]{:S(2)}, u32[]{:S(2)}) %collective-permute-start.11) | collective-permute-done | bytes 393248 | tf_op jit(solution)/shard_map/ppermute | solution.py:19
  218.3 37.7 %all-reduce.19.cloned.1.call-done = f32[2,256,256]{2,1,0:T(8,128)} async-done(((f32[2,256,256]{2,1,0:T(8,128)}), f32[2,256,256]{2,1,0:T(8,128)}) %all-reduce.19.cloned.1.call-update) | async-done | bytes 524304 | tf_op jit(solution)/shard_map/psum | solution.py:155
  258.3 1.7 convolution_convert_fusion.2
  260.0 1.5 copy.168
  263.8 7.8 dynamic_update_slice.26
  271.6 2.0 fusion.47
  273.6 8.2 %dynamic_update_slice.27 = f32[2,384,512]{1,2,0:T(8,128)S(1)} dynamic-update-slice(f32[2,384,512]{1,2,0:T(8,128)S(1)} %dynamic_update_slice.26, f32[2,256,256]{1,2,0:T(8,128)} %fusion.47, s32[]{:T(128)} %constant.15.clone.1, s32[]{:T(128)S(6)} %select_n.33, s32[]{:T(128)S(6)} %select_n.34) | dynamic-update-slice | bytes 1048580 | tf_op jit(solution)/shard_map/dynamic_update_slice | solution.py:166
  284.7 2.3 collective-permute-done.13
  287.2 3.3 collective-permute-start.14
  291.8 12.9 %collective-permute-done.14 = f32[2,640,128]{1,2,0:T(8,128)S(1)} collective-permute-done((f32[2,640,128]{1,2,0:T(8,128)S(1)}, f32[2,640,128]{1,2,0:T(8,128)S(1)}, u32[]{:S(2)}, u32[]{:S(2)}) %collective-permute-start.14) | collective-permute-done | bytes 655392 | tf_op jit(solution)/shard_map/ppermute | solution.py:16
  304.7 16.7 %collective-permute-done.15 = f32[2,640,128]{1,2,0:T(8,128)S(1)} collective-permute-done((f32[2,640,128]{1,2,0:T(8,128)S(1)}, f32[2,640,128]{1,2,0:T(8,128)S(1)}, u32[]{:S(2)}, u32[]{:S(2)}) %collective-permute-start.15) | collective-permute-done | bytes 655392 | tf_op jit(solution)/shard_map/ppermute | solution.py:19
  322.6 33.6 %all-reduce.21.cloned.1.call-done = f32[2,128,256]{1,2,0:T(8,128)} async-done(((f32[2,128,256]{1,2,0:T(8,128)}), f32[2,128,256]{1,2,0:T(8,128)}) %all-reduce.21.cloned.1.call-update) | async-done | bytes 262160 | tf_op jit(solution)/shard_map/psum | solution.py:158
  356.1 1.8 fusion.81
  357.9 40.4 %all-reduce.5 = (f32[]{:T(128)}, f32[]{:T(128)}) all-reduce(f32[]{:T(128)} %get-tuple-element.16, f32[]{:T(128)} %get-tuple-element.15), channel_id=1, replica_groups=mesh['gx'=2,'gy'=4,'ma'=4] {'gx','gy','ma'}, use_global_device_ids=true, to_apply=%region_6.7 | all-reduce | flops 2 | bytes 16 | tf_op jit(solution)/shard_map/psum | solution.py:193
  402.3 2.1 collective-permute-done.17
  404.6 4.2 collective-permute-start.18
  410.1 7.3 collective-permute-done.18
  417.4 10.6 %collective-permute-done.19 = f32[2,384,128]{1,2,0:T(8,128)S(1)} collective-permute-done((f32[2,384,128]{1,2,0:T(8,128)S(1)}, f32[2,384,128]{1,2,0:T(8,128)S(1)}, u32[]{:S(2)}, u32[]{:S(2)}) %collective-permute-start.19) | collective-permute-done | bytes 393248 | tf_op jit(solution)/shard_map/ppermute | solution.py:19
  435.4 36.2 %all-reduce.23.cloned.1.call-done = f32[2,256,256]{2,1,0:T(8,128)} async-done(((f32[2,256,256]{2,1,0:T(8,128)}), f32[2,256,256]{2,1,0:T(8,128)}) %all-reduce.23.cloned.1.call-update) | async-done | bytes 524304 | tf_op jit(solution)/shard_map/psum | solution.py:155
  474.1 1.7 convolution_convert_fusion.1
  475.8 1.5 copy.169
  479.5 7.8 dynamic_update_slice.28
  487.3 2.0 fusion.44
  489.3 8.2 %dynamic_update_slice.29 = f32[2,384,512]{1,2,0:T(8,128)S(1)} dynamic-update-slice(f32[2,384,512]{1,2,0:T(8,128)S(1)} %dynamic_update_slice.28, f32[2,256,256]{1,2,0:T(8,128)} %fusion.44, s32[]{:T(128)} %constant.15.clone.1, s32[]{:T(128)S(6)} %select_n.33, s32[]{:T(128)S(6)} %select_n.34) | dynamic-update-slice | bytes 1048580 | tf_op jit(solution)/shard_map/dynamic_update_slice | solution.py:166
  500.4 2.3 collective-permute-done.21
  502.8 3.3 collective-permute-start.22
  507.4 12.9 %collective-permute-done.22 = f32[2,640,128]{1,2,0:T(8,128)S(1)} collective-permute-done((f32[2,640,128]{1,2,0:T(8,128)S(1)}, f32[2,640,128]{1,2,0:T(8,128)S(1)}, u32[]{:S(2)}, u32[]{:S(2)}) %collective-permute-start.22) | collective-permute-done | bytes 655392 | tf_op jit(solution)/shard_map/ppermute | solution.py:16
  520.4 16.7 %collective-permute-done.23 = f32[2,640,128]{1,2,0:T(8,128)S(1)} collective-permute-done((f32[2,640,128]{1,2,0:T(8,128)S(1)}, f32[2,640,128]{1,2,0:T(8,128)S(1)}, u32[]{:S(2)}, u32[]{:S(2)}) %collective-permute-start.23) | collective-permute-done | bytes 655392 | tf_op jit(solution)/shard_map/ppermute | solution.py:19
  538.0 33.7 %all-reduce.25.cloned.1.call-done = f32[2,128,256]{1,2,0:T(8,128)} async-done(((f32[2,128,256]{1,2,0:T(8,128)}), f32[2,128,256]{1,2,0:T(8,128)}) %all-reduce.25.cloned.1.call-update) | async-done | bytes 262160 | tf_op jit(solution)/shard_map/psum | solution.py:158
  575.4 2.1 collective-permute-done.25
  577.6 3.4 collective-permute-start.26
  582.3 7.3 collective-permute-done.26
  589.6 10.3 %collective-permute-done.27 = f32[2,384,128]{1,2,0:T(8,128)S(1)} collective-permute-done((f32[2,384,128]{1,2,0:T(8,128)S(1)}, f32[2,384,128]{1,2,0:T(8,128)S(1)}, u32[]{:S(2)}, u32[]{:S(2)}) %collective-permute-start.27) | collective-permute-done | bytes 393248 | tf_op jit(solution)/shard_map/ppermute | solution.py:19
  607.7 37.7 %all-reduce.27.cloned.1.call-done = f32[2,256,256]{2,1,0:T(8,128)} async-done(((f32[2,256,256]{2,1,0:T(8,128)}), f32[2,256,256]{2,1,0:T(8,128)}) %all-reduce.27.cloned.1.call-update) | async-done | bytes 524304 | tf_op jit(solution)/shard_map/psum | solution.py:155
  647.7 1.7 convolution_convert_fusion
  649.4 1.5 copy.170
  653.0 8.2 %dynamic_update_slice.30 = f32[2,384,512]{1,2,0:T(8,128)S(1)} dynamic-update-slice(f32[2,384,512]{1,2,0:T(8,128)S(1)} %broadcast.214, f32[2,256,256]{1,2,0:T(8,128)S(1)} %fusion.25, s32[]{:T(128)} %constant.15.clone.1, s32[]{:T(128)S(6)} %select_n.31, s32[]{:T(128)S(6)} %select_n.32) | dynamic-update-slice | bytes 1048580 | tf_op jit(solution)/shard_map/dynamic_update_slice | solution.py:166
  662.4 8.8 %dynamic_update_slice.31 = f32[2,384,512]{1,2,0:T(8,128)S(1)} dynamic-update-slice(f32[2,384,512]{1,2,0:T(8,128)S(1)} %dynamic_update_slice.30, f32[2,256,256]{1,2,0:T(8,128)S(1)} %fusion.41, s32[]{:T(128)} %constant.15.clone.1, s32[]{:T(128)S(6)} %select_n.33, s32[]{:T(128)S(6)} %select_n.34) | dynamic-update-slice | bytes 1048580 | tf_op jit(solution)/shard_map/dynamic_update_slice | solution.py:166
  674.2 2.3 collective-permute-done.29
  676.6 3.2 collective-permute-start.30
  681.1 12.9 %collective-permute-done.30 = f32[2,640,128]{1,2,0:T(8,128)S(1)} collective-permute-done((f32[2,640,128]{1,2,0:T(8,128)S(1)}, f32[2,640,128]{1,2,0:T(8,128)S(1)}, u32[]{:S(2)}, u32[]{:S(2)}) %collective-permute-start.30) | collective-permute-done | bytes 655392 | tf_op jit(solution)/shard_map/ppermute | solution.py:16
  694.1 16.9 %collective-permute-done.31 = f32[2,640,128]{1,2,0:T(8,128)S(1)} collective-permute-done((f32[2,640,128]{1,2,0:T(8,128)S(1)}, f32[2,640,128]{1,2,0:T(8,128)S(1)}, u32[]{:S(2)}, u32[]{:S(2)}) %collective-permute-start.31) | collective-permute-done | bytes 655392 | tf_op jit(solution)/shard_map/ppermute | solution.py:19
  712.0 33.7 %all-reduce.29.cloned.1.call-done = f32[2,128,256]{1,2,0:T(8,128)} async-done(((f32[2,128,256]{1,2,0:T(8,128)}), f32[2,128,256]{1,2,0:T(8,128)}) %all-reduce.29.cloned.1.call-update) | async-done | bytes 262160 | tf_op jit(solution)/shard_map/psum | solution.py:158
  745.7 1.8 fusion.82
  747.6 40.4 %all-reduce.4 = (f32[]{:T(128)}, f32[]{:T(128)}) all-reduce(f32[]{:T(128)} %get-tuple-element.14, f32[]{:T(128)} %get-tuple-element.13), channel_id=1, replica_groups=mesh['gx'=2,'gy'=4,'ma'=4] {'gx','gy','ma'}, use_global_device_ids=true, to_apply=%region_20.21 | all-reduce | flops 2 | bytes 16 | tf_op jit(solution)/shard_map/psum | solution.py:193
  (232 shorter events, 92.1 us)
Async XLA Ops:
  6.5 5.2 copy-start.23
  6.5 75.1 %all-reduce.15.cloned.1.call-start = ((), (), s32[]{:S(2)}) async-start(), calls=%async_computation | async-start | bytes 1048576 | tf_op jit(solution)/shard_map/psum | solution.py:155
  6.5 5.2 collective-permute-start
  9.1 3.6 collective-permute-start.1
  11.7 7.5 copy-start.32
  13.7 17.3 %collective-permute-start.2 = (f32[2,384,128]{2,1,0:T(8,128)}, f32[2,384,128]{2,1,0:T(8,128)S(1)}, u32[]{:S(2)}, u32[]{:S(2)}) collective-permute-start(f32[2,384,128]{2,1,0:T(8,128)} %get-tuple-element.69), channel_id=1, source_target_pairs={{0,4},{4,8},{8,12},{1,5},{5,9},{9,13},{2,6},{6,10},{10,14},{3,7},{... | collective-permute-start | bytes 1179656 | tf_op jit(solution)/shard_map/ppermute | solution.py:16
  17.9 19.4 %collective-permute-start.3 = (f32[2,384,128]{2,1,0:T(8,128)}, f32[2,384,128]{2,1,0:T(8,128)}, u32[]{:S(2)}, u32[]{:S(2)}) collective-permute-start(f32[2,384,128]{2,1,0:T(8,128)} %get-tuple-element.70), channel_id=1, source_target_pairs={{4,0},{8,4},{12,8},{5,1},{9,5},{13,9},{6,2},{10,6},{14,10},{7,3},{... | collective-permute-start | bytes 1179656 | tf_op jit(solution)/shard_map/ppermute | solution.py:19
  28.3 10.1 %copy-start.18 = (bf16[512,512]{1,0:T(8,128)(2,1)}, bf16[512,512]{1,0:T(8,128)(2,1)S(1)}, u32[]{:S(2)}) copy-start(bf16[512,512]{1,0:T(8,128)(2,1)S(1)} %get-tuple-element.72) | copy-start | bytes 1572868
  28.4 11.2 %copy-start.27 = (bf16[2,256,2,256]{3,2,1,0:T(2,128)(2,1)}, bf16[2,256,2,256]{3,2,1,0:T(2,128)(2,1)S(1)}, u32[]{:S(2)}) copy-start(bf16[2,256,2,256]{3,2,1,0:T(2,128)(2,1)S(1)} %convert_element_type.132) | copy-start | bytes 1572868
  39.6 1.0 copy-start.4
  41.4 41.6 %copy-start = (f32[2,2,256,512,1]{3,2,4,1,0:T(8,128)}, f32[2,2,256,512,1]{3,2,4,1,0:T(8,128)S(1)}, u32[]{:S(2)}) copy-start(f32[2,2,256,512,1]{3,2,4,1,0:T(8,128)S(1)} %get-tuple-element.78) | copy-start | bytes 6291460
  42.5 139.8 %all-reduce.17.cloned.1.call-start = ((), (), s32[]{:S(2)}) async-start(), calls=%async_computation.1 | async-start | bytes 524288 | tf_op jit(solution)/shard_map/psum | solution.py:158
  83.0 1.0 copy-start.19
  85.7 1.5 copy-start.8
  107.6 2.8 collective-permute-start.4
  108.9 3.8 collective-permute-start.5
  112.8 17.5 %collective-permute-start.6 = (f32[2,640,128]{1,2,0:T(8,128)S(1)}, f32[2,640,128]{1,2,0:T(8,128)S(1)}, u32[]{:S(2)}, u32[]{:S(2)}) collective-permute-start(f32[2,640,128]{1,2,0:T(8,128)S(1)} %get-tuple-element.27), channel_id=1, source_target_pairs={{0,4},{4,8},{8,12},{1,5},{5,9},{9,13},{2,6},{6,10},{10,14},{3,7},{... | collective-permute-start | bytes 1966088 | tf_op jit(solution)/shard_map/ppermute | solution.py:16
  116.1 30.9 %collective-permute-start.7 = (f32[2,640,128]{1,2,0:T(8,128)S(1)}, f32[2,640,128]{1,2,0:T(8,128)S(1)}, u32[]{:S(2)}, u32[]{:S(2)}) collective-permute-start(f32[2,640,128]{1,2,0:T(8,128)S(1)} %get-tuple-element.28), channel_id=1, source_target_pairs={{4,0},{8,4},{12,8},{5,1},{9,5},{13,9},{6,2},{10,6},{14,10},{7,3},{... | collective-permute-start | bytes 1966088 | tf_op jit(solution)/shard_map/ppermute | solution.py:19
  148.5 107.5 %all-reduce.19.cloned.1.call-start = ((), (), s32[]{:S(2)}) async-start(), calls=%async_computation.2 | async-start | bytes 1048576 | tf_op jit(solution)/shard_map/psum | solution.py:155
  183.3 2.6 collective-permute-start.8
  184.6 3.4 collective-permute-start.9
  188.2 12.0 %collective-permute-start.10 = (f32[2,384,128]{1,2,0:T(8,128)S(1)}, f32[2,384,128]{1,2,0:T(8,128)S(1)}, u32[]{:S(2)}, u32[]{:S(2)}) collective-permute-start(f32[2,384,128]{1,2,0:T(8,128)S(1)} %get-tuple-element.67), channel_id=1, source_target_pairs={{0,4},{4,8},{8,12},{1,5},{5,9},{9,13},{2,6},{6,10},{10,14},{3,7},{... | collective-permute-start | bytes 1179656 | tf_op jit(solution)/shard_map/ppermute | solution.py:16
  191.6 19.0 %collective-permute-start.11 = (f32[2,384,128]{1,2,0:T(8,128)S(1)}, f32[2,384,128]{1,2,0:T(8,128)S(1)}, u32[]{:S(2)}, u32[]{:S(2)}) collective-permute-start(f32[2,384,128]{1,2,0:T(8,128)S(1)} %get-tuple-element.68), channel_id=1, source_target_pairs={{4,0},{8,4},{12,8},{5,1},{9,5},{13,9},{6,2},{10,6},{14,10},{7,3},{... | collective-permute-start | bytes 1179656 | tf_op jit(solution)/shard_map/ppermute | solution.py:19
  213.8 1.0 copy-start.28
  214.8 1.6 copy-start.1
  214.8 1.7 copy-start.5
  218.2 137.9 %all-reduce.21.cloned.1.call-start = ((), (), s32[]{:S(2)}) async-start(), calls=%async_computation.3 | async-start | bytes 524288 | tf_op jit(solution)/shard_map/psum | solution.py:158
  257.3 1.0 copy-start.20
  260.0 1.5 copy-start.9
  281.9 2.8 collective-permute-start.12
  283.3 3.8 collective-permute-start.13
  287.2 17.5 %collective-permute-start.14 = (f32[2,640,128]{1,2,0:T(8,128)S(1)}, f32[2,640,128]{1,2,0:T(8,128)S(1)}, u32[]{:S(2)}, u32[]{:S(2)}) collective-permute-start(f32[2,640,128]{1,2,0:T(8,128)S(1)} %get-tuple-element.25), channel_id=1, source_target_pairs={{0,4},{4,8},{8,12},{1,5},{5,9},{9,13},{2,6},{6,10},{10,14},{3,7},{... | collective-permute-start | bytes 1966088 | tf_op jit(solution)/shard_map/ppermute | solution.py:16
  290.5 30.9 %collective-permute-start.15 = (f32[2,640,128]{1,2,0:T(8,128)S(1)}, f32[2,640,128]{1,2,0:T(8,128)S(1)}, u32[]{:S(2)}, u32[]{:S(2)}) collective-permute-start(f32[2,640,128]{1,2,0:T(8,128)S(1)} %get-tuple-element.26), channel_id=1, source_target_pairs={{4,0},{8,4},{12,8},{5,1},{9,5},{13,9},{6,2},{10,6},{14,10},{7,3},{... | collective-permute-start | bytes 1966088 | tf_op jit(solution)/shard_map/ppermute | solution.py:19
  321.5 78.1 %copy-start.25 = (f32[2,128,256]{1,2,0:T(8,128)S(1)}, f32[2,128,256]{1,2,0:T(8,128)}, u32[]{:S(2)}) copy-start(f32[2,128,256]{1,2,0:T(8,128)} %all-reduce.17.cloned.1.call-done) | copy-start | bytes 786436
  322.4 149.3 %all-reduce.23.cloned.1.call-start = ((), (), s32[]{:S(2)}) async-start(), calls=%async_computation.4 | async-start | bytes 1048576 | tf_op jit(solution)/shard_map/psum | solution.py:155
  399.7 28.3 %copy-start.16 = (f32[2,128,256]{1,2,0:T(8,128)}, f32[2,128,256]{1,2,0:T(8,128)S(1)}, u32[]{:S(2)}) copy-start(f32[2,128,256]{1,2,0:T(8,128)S(1)} %multiply_add_fusion.1) | copy-start | bytes 786436
  399.7 2.6 collective-permute-start.16
  401.0 3.4 collective-permute-start.17
  404.6 12.8 %collective-permute-start.18 = (f32[2,384,128]{1,2,0:T(8,128)S(1)}, f32[2,384,128]{1,2,0:T(8,128)S(1)}, u32[]{:S(2)}, u32[]{:S(2)}) collective-permute-start(f32[2,384,128]{1,2,0:T(8,128)S(1)} %get-tuple-element.65), channel_id=1, source_target_pairs={{0,4},{4,8},{8,12},{1,5},{5,9},{9,13},{2,6},{6,10},{10,14},{3,7},{... | collective-permute-start | bytes 1179656 | tf_op jit(solution)/shard_map/ppermute | solution.py:16
  408.8 19.2 %collective-permute-start.19 = (f32[2,384,128]{1,2,0:T(8,128)S(1)}, f32[2,384,128]{1,2,0:T(8,128)S(1)}, u32[]{:S(2)}, u32[]{:S(2)}) collective-permute-start(f32[2,384,128]{1,2,0:T(8,128)S(1)} %get-tuple-element.66), channel_id=1, source_target_pairs={{4,0},{8,4},{12,8},{5,1},{9,5},{13,9},{6,2},{10,6},{14,10},{7,3},{... | collective-permute-start | bytes 1179656 | tf_op jit(solution)/shard_map/ppermute | solution.py:19
  431.2 1.0 copy-start.29
  434.0 39.0 %copy-start.2 = (f32[2,2,256,512,1]{3,2,4,1,0:T(8,128)}, f32[2,2,256,512,1]{3,2,4,1,0:T(8,128)S(1)}, u32[]{:S(2)}) copy-start(f32[2,2,256,512,1]{3,2,4,1,0:T(8,128)S(1)} %get-tuple-element.80) | copy-start | bytes 6291460
  435.1 136.6 %all-reduce.25.cloned.1.call-start = ((), (), s32[]{:S(2)}) async-start(), calls=%async_computation.5 | async-start | bytes 524288 | tf_op jit(solution)/shard_map/psum | solution.py:158
  473.0 1.0 copy-start.21
  475.8 1.5 copy-start.10
  497.6 2.8 collective-permute-start.20
  498.9 3.8 collective-permute-start.21
  502.8 17.5 %collective-permute-start.22 = (f32[2,640,128]{1,2,0:T(8,128)S(1)}, f32[2,640,128]{1,2,0:T(8,128)S(1)}, u32[]{:S(2)}, u32[]{:S(2)}) collective-permute-start(f32[2,640,128]{1,2,0:T(8,128)S(1)} %get-tuple-element.23), channel_id=1, source_target_pairs={{0,4},{4,8},{8,12},{1,5},{5,9},{9,13},{2,6},{6,10},{10,14},{3,7},{... | collective-permute-start | bytes 1966088 | tf_op jit(solution)/shard_map/ppermute | solution.py:16
  506.1 30.9 %collective-permute-start.23 = (f32[2,640,128]{1,2,0:T(8,128)S(1)}, f32[2,640,128]{1,2,0:T(8,128)S(1)}, u32[]{:S(2)}, u32[]{:S(2)}) collective-permute-start(f32[2,640,128]{1,2,0:T(8,128)S(1)} %get-tuple-element.24), channel_id=1, source_target_pairs={{4,0},{8,4},{12,8},{5,1},{9,5},{13,9},{6,2},{10,6},{14,10},{7,3},{... | collective-permute-start | bytes 1966088 | tf_op jit(solution)/shard_map/ppermute | solution.py:19
  538.0 107.5 %all-reduce.27.cloned.1.call-start = ((), (), s32[]{:S(2)}) async-start(), calls=%async_computation.6 | async-start | bytes 1048576 | tf_op jit(solution)/shard_map/psum | solution.py:155
  572.7 2.6 collective-permute-start.24
  574.0 3.4 collective-permute-start.25
  577.6 12.0 %collective-permute-start.26 = (f32[2,384,128]{1,2,0:T(8,128)S(1)}, f32[2,384,128]{1,2,0:T(8,128)S(1)}, u32[]{:S(2)}, u32[]{:S(2)}) collective-permute-start(f32[2,384,128]{1,2,0:T(8,128)S(1)} %get-tuple-element.63), channel_id=1, source_target_pairs={{0,4},{4,8},{8,12},{1,5},{5,9},{9,13},{2,6},{6,10},{10,14},{3,7},{... | collective-permute-start | bytes 1179656 | tf_op jit(solution)/shard_map/ppermute | solution.py:16
  581.0 19.0 %collective-permute-start.27 = (f32[2,384,128]{1,2,0:T(8,128)S(1)}, f32[2,384,128]{1,2,0:T(8,128)S(1)}, u32[]{:S(2)}, u32[]{:S(2)}) collective-permute-start(f32[2,384,128]{1,2,0:T(8,128)S(1)} %get-tuple-element.64), channel_id=1, source_target_pairs={{4,0},{8,4},{12,8},{5,1},{9,5},{13,9},{6,2},{10,6},{14,10},{7,3},{... | collective-permute-start | bytes 1179656 | tf_op jit(solution)/shard_map/ppermute | solution.py:19
  604.3 1.6 copy-start.3
  604.3 1.7 copy-start.7
  607.7 138.1 %all-reduce.29.cloned.1.call-start = ((), (), s32[]{:S(2)}) async-start(), calls=%async_computation.7 | async-start | bytes 524288 | tf_op jit(solution)/shard_map/psum | solution.py:158
  649.4 1.5 copy-start.11
  671.3 2.8 collective-permute-start.28
  672.7 3.8 collective-permute-start.29
  676.6 17.5 %collective-permute-start.30 = (f32[2,640,128]{1,2,0:T(8,128)S(1)}, f32[2,640,128]{1,2,0:T(8,128)S(1)}, u32[]{:S(2)}, u32[]{:S(2)}) collective-permute-start(f32[2,640,128]{1,2,0:T(8,128)S(1)} %get-tuple-element.21), channel_id=1, source_target_pairs={{0,4},{4,8},{8,12},{1,5},{5,9},{9,13},{2,6},{6,10},{10,14},{3,7},{... | collective-permute-start | bytes 1966088 | tf_op jit(solution)/shard_map/ppermute | solution.py:16
  679.8 31.2 %collective-permute-start.31 = (f32[2,640,128]{1,2,0:T(8,128)S(1)}, f32[2,640,128]{1,2,0:T(8,128)S(1)}, u32[]{:S(2)}, u32[]{:S(2)}) collective-permute-start(f32[2,640,128]{1,2,0:T(8,128)S(1)} %get-tuple-element.22), channel_id=1, source_target_pairs={{4,0},{8,4},{12,8},{5,1},{9,5},{13,9},{6,2},{10,6},{14,10},{7,3},{... | collective-permute-start | bytes 1966088 | tf_op jit(solution)/shard_map/ppermute | solution.py:19
  711.1 78.2 %copy-start.17 = (f32[2,128,256]{1,2,0:T(8,128)S(1)}, f32[2,128,256]{1,2,0:T(8,128)}, u32[]{:S(2)}) copy-start(f32[2,128,256]{1,2,0:T(8,128)} %copy-done.16) | copy-start | bytes 786436
  711.1 78.2 %copy-start.26 = (f32[2,128,256]{1,2,0:T(8,128)S(1)}, f32[2,128,256]{1,2,0:T(8,128)}, u32[]{:S(2)}) copy-start(f32[2,128,256]{1,2,0:T(8,128)} %all-reduce.25.cloned.1.call-done) | copy-start | bytes 786436
  (9 other events, 8.6 us)
Sparse Core Ops, SparseCore 0:
  42.6 38.9 all-reduce.14
  148.7 33.5 all-reduce.16
  218.4 37.6 all-reduce.18
  322.5 33.5 all-reduce.20
  435.2 36.3 all-reduce.22
  538.1 33.5 all-reduce.24
  607.8 37.6 all-reduce.26
  712.1 33.5 all-reduce.28
where the time goes:
time: 808 us; the launch traced here: 797 us
  waiting for transfers between devices  478 us (59%)
  local copies, waits for them, and re-layouts  94.4 us (12%)
  blocking collectives  80.8 us (10%)
  starting transfers between devices  61.5 us (8%)
  other arithmetic  40.6 us (5%)
  between operations  26.1 us (3%)
  matrix products  15.7 us (2%)
    psum x4, waiting for transfers between devices, mode_total(): return lax.psum(partial_value, 'ma')  148 us
    psum x4, waiting for transfers between devices, combine(): summed = lax.psum(folded, 'ma')  135 us
    ppermute x16, waiting for transfers between devices, padded_2(): lax.ppermute(lax.slice_in_dim(block, 0, width, axis=dim), axis, backward)  121 us
    psum x2, blocking collectives, shards(): norm_now = lax.psum(local_sum(residual, residual), ('gx', 'gy', 'ma'))  80.8 us
    ppermute x16, waiting for transfers between devices, padded_2(): lax.ppermute(lax.slice_in_dim(block, block.shape[dim] - width, None, axis...  74.3 us
    dynamic_update_slice x8, local copies, waits for them, and re-layouts, project(): lax.dynamic_update_slice(extended, lax.dynamic_slice(extended, corner, (2...  65.2 us
    ppermute x16, starting transfers between devices, padded_2(): lax.ppermute(lax.slice_in_dim(block, block.shape[dim] - width, None, axis...  40.1 us
    ppermute x16, starting transfers between devices, padded_2(): lax.ppermute(lax.slice_in_dim(block, 0, width, axis=dim), axis, backward)  20.8 us
  transfers between devices with their start and end apart: 40, of which 35 were waited for; matrix products, arithmetic and copies ran while one was open for 1% of the time, Pallas kernels for 0%

commit v1 on v0

--- a/solution.py
+++ b/solution.py
@@ -190,7 +190,7 @@
         gradient = project(misfit, spectra)
         residual = -gradient
         direction = residual
-        norm_now = lax.psum(local_sum(residual, residual), ("gx", "gy", "ma"))
+        norm_now = lax.psum(lax.psum(local_sum(residual, residual), ("gy", "ma")), "gx")
         moved_spectra = spectra_of(direction)
         change = live_mask * mode_total(change_part(spectra, moved_spectra, mode_count))
         applied = project(change, spectra) + DAMPING * direction

time: 808 us -> 892 us (1.10)
  blocking collectives: 80.8 us -> 163 us
    psum x2 -> x6, blocking collectives: 80.8 us -> 163 us  [the longest x2 82.9 us: shards(): lax.psum(local_sum(residual, residual), ('gy', 'ma'))]
where the time goes in v1:
time: 892 us; the launch traced here: 881 us
  waiting for transfers between devices  479 us (54%)
  blocking collectives  163 us (18%)
  local copies, waits for them, and re-layouts  94.5 us (11%)
  starting transfers between devices  61.4 us (7%)
  other arithmetic  40.5 us (5%)
  between operations  26 us (3%)
  matrix products  15.7 us (2%)
    psum x4, waiting for transfers between devices, mode_total(): return lax.psum(partial_value, 'ma')  149 us
    psum x4, waiting for transfers between devices, combine(): summed = lax.psum(folded, 'ma')  135 us
    ppermute x16, waiting for transfers between devices, padded_2(): lax.ppermute(lax.slice_in_dim(block, 0, width, axis=dim), axis, backward)  121 us
    psum x2, blocking collectives, shards(): lax.psum(local_sum(residual, residual), ('gy', 'ma'))  82.9 us
    ppermute x16, waiting for transfers between devices, padded_2(): lax.ppermute(lax.slice_in_dim(block, block.shape[dim] - width, None, axis...  74.3 us
    psum x2, blocking collectives, shards(): lax.psum(local_sum(direction, applied), ('gx', 'gy', 'ma'))  74 us
    dynamic_update_slice x8, local copies, waits for them, and re-layouts, project(): lax.dynamic_update_slice(extended, lax.dynamic_slice(extended, corner, (2...  65.2 us
    ppermute x16, starting transfers between devices, padded_2(): lax.ppermute(lax.slice_in_dim(block, block.shape[dim] - width, None, axis...  40.1 us
  transfers between devices with their start and end apart: 40, of which 35 were waited for; matrix products, arithmetic and copies ran while one was open for 1% of the time, Pallas kernels for 0%

profile of v1, /device:TPU:0, one launch (start us, length us, event | category | flops | bytes accessed | tf_op | source)
XLA Modules:
  0.0 880.6 jit_solution(12997406391595646566)
XLA Ops:
  6.5 2.5 collective-permute-start
  13.7 4.2 collective-permute-start.2
  31.1 6.2 collective-permute-done.3
  42.5 2.0 convert_element_type.140
  45.2 36.4 %all-reduce.13.cloned.1.call-done = f32[2,256,256]{2,1,0:T(8,128)} async-done(((f32[2,256,256]{2,1,0:T(8,128)}), f32[2,256,256]{2,1,0:T(8,128)}) %all-reduce.13.cloned.1.call-update) | async-done | bytes 524304 | tf_op jit(solution)/shard_map/psum | solution.py:155
  84.1 1.7 convolution_convert_fusion.3
  85.8 1.5 copy.167
  89.6 7.8 dynamic_update_slice.24
  97.4 2.0 fusion.50
  99.4 8.2 dynamic_update_slice.25
  110.5 2.3 collective-permute-done.5
  112.9 3.3 collective-permute-start.6
  117.5 12.9 %collective-permute-done.6 = f32[2,640,128]{1,2,0:T(8,128)S(1)} collective-permute-done((f32[2,640,128]{1,2,0:T(8,128)S(1)}, f32[2,640,128]{1,2,0:T(8,128)S(1)}, u32[]{:S(2)}, u32[]{:S(2)}) %collective-permute-start.6) | collective-permute-done | bytes 655392 | tf_op jit(solution)/shard_map/ppermute | solution.py:16
  130.5 16.7 %collective-permute-done.7 = f32[2,640,128]{1,2,0:T(8,128)S(1)} collective-permute-done((f32[2,640,128]{1,2,0:T(8,128)S(1)}, f32[2,640,128]{1,2,0:T(8,128)S(1)}, u32[]{:S(2)}, u32[]{:S(2)}) %collective-permute-start.7) | collective-permute-done | bytes 655392 | tf_op jit(solution)/shard_map/ppermute | solution.py:19
  148.7 33.7 %all-reduce.15.cloned.1.call-done = f32[2,128,256]{1,2,0:T(8,128)} async-done(((f32[2,128,256]{1,2,0:T(8,128)}), f32[2,128,256]{1,2,0:T(8,128)}) %all-reduce.15.cloned.1.call-update) | async-done | bytes 262160 | tf_op jit(solution)/shard_map/psum | solution.py:158
  186.0 2.1 collective-permute-done.9
  188.2 3.4 collective-permute-start.10
  193.1 7.2 collective-permute-done.10
  200.3 10.3 %collective-permute-done.11 = f32[2,384,128]{1,2,0:T(8,128)S(1)} collective-permute-done((f32[2,384,128]{1,2,0:T(8,128)S(1)}, f32[2,384,128]{1,2,0:T(8,128)S(1)}, u32[]{:S(2)}, u32[]{:S(2)}) %collective-permute-start.11) | collective-permute-done | bytes 393248 | tf_op jit(solution)/shard_map/ppermute | solution.py:19
  218.4 37.7 %all-reduce.17.cloned.1.call-done = f32[2,256,256]{2,1,0:T(8,128)} async-done(((f32[2,256,256]{2,1,0:T(8,128)}), f32[2,256,256]{2,1,0:T(8,128)}) %all-reduce.17.cloned.1.call-update) | async-done | bytes 524304 | tf_op jit(solution)/shard_map/psum | solution.py:155
  258.4 1.7 convolution_convert_fusion.2
  263.8 7.8 dynamic_update_slice.26
  271.7 2.0 fusion.47
  273.6 8.2 dynamic_update_slice.27
  284.8 2.3 collective-permute-done.13
  287.2 3.3 collective-permute-start.14
  291.8 12.9 %collective-permute-done.14 = f32[2,640,128]{1,2,0:T(8,128)S(1)} collective-permute-done((f32[2,640,128]{1,2,0:T(8,128)S(1)}, f32[2,640,128]{1,2,0:T(8,128)S(1)}, u32[]{:S(2)}, u32[]{:S(2)}) %collective-permute-start.14) | collective-permute-done | bytes 655392 | tf_op jit(solution)/shard_map/ppermute | solution.py:16
  304.7 16.7 %collective-permute-done.15 = f32[2,640,128]{1,2,0:T(8,128)S(1)} collective-permute-done((f32[2,640,128]{1,2,0:T(8,128)S(1)}, f32[2,640,128]{1,2,0:T(8,128)S(1)}, u32[]{:S(2)}, u32[]{:S(2)}) %collective-permute-start.15) | collective-permute-done | bytes 655392 | tf_op jit(solution)/shard_map/ppermute | solution.py:19
  322.4 33.7 %all-reduce.19.cloned.1.call-done = f32[2,128,256]{1,2,0:T(8,128)} async-done(((f32[2,128,256]{1,2,0:T(8,128)}), f32[2,128,256]{1,2,0:T(8,128)}) %all-reduce.19.cloned.1.call-update) | async-done | bytes 262160 | tf_op jit(solution)/shard_map/psum | solution.py:158
  356.1 1.8 fusion.81
  357.9 41.4 %psum.100 = f32[]{:T(128)} all-reduce(f32[]{:T(128)} %get-tuple-element.16), channel_id=1, replica_groups=mesh['gx'=2,'gy'=4,'ma'=4] {'gy','ma'}, use_global_device_ids=true, to_apply=%region_6.7 | all-reduce | flops 1 | bytes 8 | tf_op jit(solution)/shard_map/psum | solution.py:193
  399.5 3.0 psum.101
  402.4 37.0 %psum.104 = f32[]{:T(128)} all-reduce(f32[]{:T(128)} %get-tuple-element.15), channel_id=1, replica_groups=mesh['gx'=2,'gy'=4,'ma'=4] {'gx','gy','ma'}, use_global_device_ids=true, to_apply=%region_14.15 | all-reduce | flops 1 | bytes 8 | tf_op jit(solution)/shard_map/psum | solution.py:197
  443.4 2.1 collective-permute-done.17
  445.6 4.2 collective-permute-start.18
  451.1 7.3 collective-permute-done.18
  458.5 10.5 %collective-permute-done.19 = f32[2,384,128]{1,2,0:T(8,128)S(1)} collective-permute-done((f32[2,384,128]{1,2,0:T(8,128)S(1)}, f32[2,384,128]{1,2,0:T(8,128)S(1)}, u32[]{:S(2)}, u32[]{:S(2)}) %collective-permute-start.19) | collective-permute-done | bytes 393248 | tf_op jit(solution)/shard_map/ppermute | solution.py:19
  476.4 37.3 %all-reduce.21.cloned.1.call-done = f32[2,256,256]{2,1,0:T(8,128)} async-done(((f32[2,256,256]{2,1,0:T(8,128)}), f32[2,256,256]{2,1,0:T(8,128)}) %all-reduce.21.cloned.1.call-update) | async-done | bytes 524304 | tf_op jit(solution)/shard_map/psum | solution.py:155
  516.1 1.7 convolution_convert_fusion.1
  521.6 7.8 dynamic_update_slice.28
  529.4 2.0 fusion.44
  531.4 8.2 dynamic_update_slice.29
  542.5 2.3 collective-permute-done.21
  544.9 3.3 collective-permute-start.22
  549.5 12.9 %collective-permute-done.22 = f32[2,640,128]{1,2,0:T(8,128)S(1)} collective-permute-done((f32[2,640,128]{1,2,0:T(8,128)S(1)}, f32[2,640,128]{1,2,0:T(8,128)S(1)}, u32[]{:S(2)}, u32[]{:S(2)}) %collective-permute-start.22) | collective-permute-done | bytes 655392 | tf_op jit(solution)/shard_map/ppermute | solution.py:16
  562.5 16.7 %collective-permute-done.23 = f32[2,640,128]{1,2,0:T(8,128)S(1)} collective-permute-done((f32[2,640,128]{1,2,0:T(8,128)S(1)}, f32[2,640,128]{1,2,0:T(8,128)S(1)}, u32[]{:S(2)}, u32[]{:S(2)}) %collective-permute-start.23) | collective-permute-done | bytes 655392 | tf_op jit(solution)/shard_map/ppermute | solution.py:19
  580.2 33.7 %all-reduce.23.cloned.1.call-done = f32[2,128,256]{1,2,0:T(8,128)} async-done(((f32[2,128,256]{1,2,0:T(8,128)}), f32[2,128,256]{1,2,0:T(8,128)}) %all-reduce.23.cloned.1.call-update) | async-done | bytes 262160 | tf_op jit(solution)/shard_map/psum | solution.py:158
  617.5 2.1 collective-permute-done.25
  619.7 3.4 collective-permute-start.26
  624.4 7.3 collective-permute-done.26
  631.8 10.3 %collective-permute-done.27 = f32[2,384,128]{1,2,0:T(8,128)S(1)} collective-permute-done((f32[2,384,128]{1,2,0:T(8,128)S(1)}, f32[2,384,128]{1,2,0:T(8,128)S(1)}, u32[]{:S(2)}, u32[]{:S(2)}) %collective-permute-start.27) | collective-permute-done | bytes 393248 | tf_op jit(solution)/shard_map/ppermute | solution.py:19
  649.8 37.7 %all-reduce.25.cloned.1.call-done = f32[2,256,256]{2,1,0:T(8,128)} async-done(((f32[2,256,256]{2,1,0:T(8,128)}), f32[2,256,256]{2,1,0:T(8,128)}) %all-reduce.25.cloned.1.call-update) | async-done | bytes 524304 | tf_op jit(solution)/shard_map/psum | solution.py:155
  689.8 1.7 convolution_convert_fusion
  695.1 8.2 dynamic_update_slice.30
  704.5 8.8 %dynamic_update_slice.31 = f32[2,384,512]{1,2,0:T(8,128)S(1)} dynamic-update-slice(f32[2,384,512]{1,2,0:T(8,128)S(1)} %dynamic_update_slice.30, f32[2,256,256]{1,2,0:T(8,128)S(1)} %fusion.41, s32[]{:T(128)} %constant.15.clone.1, s32[]{:T(128)S(6)} %select_n.33, s32[]{:T(128)S(6)} %select_n.34) | dynamic-update-slice | bytes 1048580 | tf_op jit(solution)/shard_map/dynamic_update_slice | solution.py:166
  716.2 2.3 collective-permute-done.29
  718.6 3.2 collective-permute-start.30
  723.2 12.9 %collective-permute-done.30 = f32[2,640,128]{1,2,0:T(8,128)S(1)} collective-permute-done((f32[2,640,128]{1,2,0:T(8,128)S(1)}, f32[2,640,128]{1,2,0:T(8,128)S(1)}, u32[]{:S(2)}, u32[]{:S(2)}) %collective-permute-start.30) | collective-permute-done | bytes 655392 | tf_op jit(solution)/shard_map/ppermute | solution.py:16
  736.1 16.9 %collective-permute-done.31 = f32[2,640,128]{1,2,0:T(8,128)S(1)} collective-permute-done((f32[2,640,128]{1,2,0:T(8,128)S(1)}, f32[2,640,128]{1,2,0:T(8,128)S(1)}, u32[]{:S(2)}, u32[]{:S(2)}) %collective-permute-start.31) | collective-permute-done | bytes 655392 | tf_op jit(solution)/shard_map/ppermute | solution.py:19
  754.0 33.8 %all-reduce.27.cloned.1.call-done = f32[2,128,256]{1,2,0:T(8,128)} async-done(((f32[2,128,256]{1,2,0:T(8,128)}), f32[2,128,256]{1,2,0:T(8,128)}) %all-reduce.27.cloned.1.call-update) | async-done | bytes 262160 | tf_op jit(solution)/shard_map/psum | solution.py:158
  787.8 1.8 fusion.82
  789.6 41.5 %psum.107 = f32[]{:T(128)} all-reduce(f32[]{:T(128)} %get-tuple-element.14), channel_id=1, replica_groups=mesh['gx'=2,'gy'=4,'ma'=4] {'gy','ma'}, use_global_device_ids=true, to_apply=%region_21.22 | all-reduce | flops 1 | bytes 8 | tf_op jit(solution)/shard_map/psum | solution.py:193
  831.1 3.1 psum.108
  834.3 37.0 %psum.111 = f32[]{:T(128)} all-reduce(f32[]{:T(128)} %get-tuple-element.13), channel_id=1, replica_groups=mesh['gx'=2,'gy'=4,'ma'=4] {'gx','gy','ma'}, use_global_device_ids=true, to_apply=%region_29.30 | all-reduce | flops 1 | bytes 8 | tf_op jit(solution)/shard_map/psum | solution.py:197
  (236 shorter events, 98.1 us)
Async XLA Ops:
  6.5 5.2 copy-start.23
  6.5 75.1 %all-reduce.13.cloned.1.call-start = ((), (), s32[]{:S(2)}) async-start(), calls=%async_computation | async-start | bytes 1048576 | tf_op jit(solution)/shard_map/psum | solution.py:155
  6.5 5.2 collective-permute-start
  9.1 3.6 collective-permute-start.1
  11.7 7.5 copy-start.32
  13.7 17.4 %collective-permute-start.2 = (f32[2,384,128]{2,1,0:T(8,128)}, f32[2,384,128]{2,1,0:T(8,128)S(1)}, u32[]{:S(2)}, u32[]{:S(2)}) collective-permute-start(f32[2,384,128]{2,1,0:T(8,128)} %get-tuple-element.65), channel_id=1, source_target_pairs={{0,4},{4,8},{8,12},{1,5},{5,9},{9,13},{2,6},{6,10},{10,14},{3,7},{... | collective-permute-start | bytes 1179656 | tf_op jit(solution)/shard_map/ppermute | solution.py:16
  17.9 19.4 %collective-permute-start.3 = (f32[2,384,128]{2,1,0:T(8,128)}, f32[2,384,128]{2,1,0:T(8,128)}, u32[]{:S(2)}, u32[]{:S(2)}) collective-permute-start(f32[2,384,128]{2,1,0:T(8,128)} %get-tuple-element.66), channel_id=1, source_target_pairs={{4,0},{8,4},{12,8},{5,1},{9,5},{13,9},{6,2},{10,6},{14,10},{7,3},{... | collective-permute-start | bytes 1179656 | tf_op jit(solution)/shard_map/ppermute | solution.py:19
  28.4 10.1 %copy-start.18 = (bf16[512,512]{1,0:T(8,128)(2,1)}, bf16[512,512]{1,0:T(8,128)(2,1)S(1)}, u32[]{:S(2)}) copy-start(bf16[512,512]{1,0:T(8,128)(2,1)S(1)} %get-tuple-element.68) | copy-start | bytes 1572868
  28.5 11.1 %copy-start.27 = (bf16[2,256,2,256]{3,2,1,0:T(2,128)(2,1)}, bf16[2,256,2,256]{3,2,1,0:T(2,128)(2,1)S(1)}, u32[]{:S(2)}) copy-start(bf16[2,256,2,256]{3,2,1,0:T(2,128)(2,1)S(1)} %convert_element_type.132) | copy-start | bytes 1572868
  39.6 1.0 copy-start.4
  41.4 41.6 %copy-start = (f32[2,2,256,512,1]{3,2,4,1,0:T(8,128)}, f32[2,2,256,512,1]{3,2,4,1,0:T(8,128)S(1)}, u32[]{:S(2)}) copy-start(f32[2,2,256,512,1]{3,2,4,1,0:T(8,128)S(1)} %get-tuple-element.74) | copy-start | bytes 6291460
  42.5 139.9 %all-reduce.15.cloned.1.call-start = ((), (), s32[]{:S(2)}) async-start(), calls=%async_computation.1 | async-start | bytes 524288 | tf_op jit(solution)/shard_map/psum | solution.py:158
  83.1 1.0 copy-start.19
  85.8 1.5 copy-start.8
  107.7 2.8 collective-permute-start.4
  109.0 3.8 collective-permute-start.5
  112.9 17.5 %collective-permute-start.6 = (f32[2,640,128]{1,2,0:T(8,128)S(1)}, f32[2,640,128]{1,2,0:T(8,128)S(1)}, u32[]{:S(2)}, u32[]{:S(2)}) collective-permute-start(f32[2,640,128]{1,2,0:T(8,128)S(1)} %get-tuple-element.23), channel_id=1, source_target_pairs={{0,4},{4,8},{8,12},{1,5},{5,9},{9,13},{2,6},{6,10},{10,14},{3,7},{... | collective-permute-start | bytes 1966088 | tf_op jit(solution)/shard_map/ppermute | solution.py:16
  116.2 30.9 %collective-permute-start.7 = (f32[2,640,128]{1,2,0:T(8,128)S(1)}, f32[2,640,128]{1,2,0:T(8,128)S(1)}, u32[]{:S(2)}, u32[]{:S(2)}) collective-permute-start(f32[2,640,128]{1,2,0:T(8,128)S(1)} %get-tuple-element.24), channel_id=1, source_target_pairs={{4,0},{8,4},{12,8},{5,1},{9,5},{13,9},{6,2},{10,6},{14,10},{7,3},{... | collective-permute-start | bytes 1966088 | tf_op jit(solution)/shard_map/ppermute | solution.py:19
  148.6 107.5 %all-reduce.17.cloned.1.call-start = ((), (), s32[]{:S(2)}) async-start(), calls=%async_computation.2 | async-start | bytes 1048576 | tf_op jit(solution)/shard_map/psum | solution.py:155
  183.4 2.6 collective-permute-start.8
  184.7 3.4 collective-permute-start.9
  188.2 12.0 %collective-permute-start.10 = (f32[2,384,128]{1,2,0:T(8,128)S(1)}, f32[2,384,128]{1,2,0:T(8,128)S(1)}, u32[]{:S(2)}, u32[]{:S(2)}) collective-permute-start(f32[2,384,128]{1,2,0:T(8,128)S(1)} %get-tuple-element.63), channel_id=1, source_target_pairs={{0,4},{4,8},{8,12},{1,5},{5,9},{9,13},{2,6},{6,10},{10,14},{3,7},{... | collective-permute-start | bytes 1179656 | tf_op jit(solution)/shard_map/ppermute | solution.py:16
  191.6 19.0 %collective-permute-start.11 = (f32[2,384,128]{1,2,0:T(8,128)S(1)}, f32[2,384,128]{1,2,0:T(8,128)S(1)}, u32[]{:S(2)}, u32[]{:S(2)}) collective-permute-start(f32[2,384,128]{1,2,0:T(8,128)S(1)} %get-tuple-element.64), channel_id=1, source_target_pairs={{4,0},{8,4},{12,8},{5,1},{9,5},{13,9},{6,2},{10,6},{14,10},{7,3},{... | collective-permute-start | bytes 1179656 | tf_op jit(solution)/shard_map/ppermute | solution.py:19
  214.9 1.6 copy-start.1
  214.9 1.7 copy-start.5
  218.3 137.8 %all-reduce.19.cloned.1.call-start = ((), (), s32[]{:S(2)}) async-start(), calls=%async_computation.3 | async-start | bytes 524288 | tf_op jit(solution)/shard_map/psum | solution.py:158
  260.1 1.5 copy-start.9
  281.9 2.8 collective-permute-start.12
  283.3 3.8 collective-permute-start.13
  287.2 17.5 %collective-permute-start.14 = (f32[2,640,128]{1,2,0:T(8,128)S(1)}, f32[2,640,128]{1,2,0:T(8,128)S(1)}, u32[]{:S(2)}, u32[]{:S(2)}) collective-permute-start(f32[2,640,128]{1,2,0:T(8,128)S(1)} %get-tuple-element.21), channel_id=1, source_target_pairs={{0,4},{4,8},{8,12},{1,5},{5,9},{9,13},{2,6},{6,10},{10,14},{3,7},{... | collective-permute-start | bytes 1966088 | tf_op jit(solution)/shard_map/ppermute | solution.py:16
  290.5 30.9 %collective-permute-start.15 = (f32[2,640,128]{1,2,0:T(8,128)S(1)}, f32[2,640,128]{1,2,0:T(8,128)S(1)}, u32[]{:S(2)}, u32[]{:S(2)}) collective-permute-start(f32[2,640,128]{1,2,0:T(8,128)S(1)} %get-tuple-element.22), channel_id=1, source_target_pairs={{4,0},{8,4},{12,8},{5,1},{9,5},{13,9},{6,2},{10,6},{14,10},{7,3},{... | collective-permute-start | bytes 1966088 | tf_op jit(solution)/shard_map/ppermute | solution.py:19
  321.5 77.8 %copy-start.24 = (f32[2,128,256]{2,1,0:T(8,128)S(1)}, f32[2,128,256]{2,1,0:T(8,128)}, u32[]{:S(2)}) copy-start(f32[2,128,256]{2,1,0:T(8,128)} %param.5) | copy-start | bytes 786436
  321.5 119.2 %copy-start.25 = (f32[2,128,256]{1,2,0:T(8,128)S(1)}, f32[2,128,256]{1,2,0:T(8,128)}, u32[]{:S(2)}) copy-start(f32[2,128,256]{1,2,0:T(8,128)} %all-reduce.15.cloned.1.call-done) | copy-start | bytes 786436
  322.4 191.3 %all-reduce.21.cloned.1.call-start = ((), (), s32[]{:S(2)}) async-start(), calls=%async_computation.4 | async-start | bytes 1048576 | tf_op jit(solution)/shard_map/psum | solution.py:155
  440.8 28.3 %copy-start.16 = (f32[2,128,256]{1,2,0:T(8,128)}, f32[2,128,256]{1,2,0:T(8,128)S(1)}, u32[]{:S(2)}) copy-start(f32[2,128,256]{1,2,0:T(8,128)S(1)} %multiply_add_fusion.1) | copy-start | bytes 786436
  440.8 2.6 collective-permute-start.16
  442.1 3.4 collective-permute-start.17
  445.6 12.8 %collective-permute-start.18 = (f32[2,384,128]{1,2,0:T(8,128)S(1)}, f32[2,384,128]{1,2,0:T(8,128)S(1)}, u32[]{:S(2)}, u32[]{:S(2)}) collective-permute-start(f32[2,384,128]{1,2,0:T(8,128)S(1)} %get-tuple-element.61), channel_id=1, source_target_pairs={{0,4},{4,8},{8,12},{1,5},{5,9},{9,13},{2,6},{6,10},{10,14},{3,7},{... | collective-permute-start | bytes 1179656 | tf_op jit(solution)/shard_map/ppermute | solution.py:16
  449.8 19.2 %collective-permute-start.19 = (f32[2,384,128]{1,2,0:T(8,128)S(1)}, f32[2,384,128]{1,2,0:T(8,128)S(1)}, u32[]{:S(2)}, u32[]{:S(2)}) collective-permute-start(f32[2,384,128]{1,2,0:T(8,128)S(1)} %get-tuple-element.62), channel_id=1, source_target_pairs={{4,0},{8,4},{12,8},{5,1},{9,5},{13,9},{6,2},{10,6},{14,10},{7,3},{... | collective-permute-start | bytes 1179656 | tf_op jit(solution)/shard_map/ppermute | solution.py:19
  472.2 1.0 copy-start.29
  475.0 40.0 %copy-start.2 = (f32[2,2,256,512,1]{3,2,4,1,0:T(8,128)}, f32[2,2,256,512,1]{3,2,4,1,0:T(8,128)S(1)}, u32[]{:S(2)}) copy-start(f32[2,2,256,512,1]{3,2,4,1,0:T(8,128)S(1)} %get-tuple-element.76) | copy-start | bytes 6291460
  476.1 137.8 %all-reduce.23.cloned.1.call-start = ((), (), s32[]{:S(2)}) async-start(), calls=%async_computation.5 | async-start | bytes 524288 | tf_op jit(solution)/shard_map/psum | solution.py:158
  517.8 1.5 copy-start.10
  539.7 2.8 collective-permute-start.20
  541.0 3.8 collective-permute-start.21
  544.9 17.5 %collective-permute-start.22 = (f32[2,640,128]{1,2,0:T(8,128)S(1)}, f32[2,640,128]{1,2,0:T(8,128)S(1)}, u32[]{:S(2)}, u32[]{:S(2)}) collective-permute-start(f32[2,640,128]{1,2,0:T(8,128)S(1)} %get-tuple-element.19), channel_id=1, source_target_pairs={{0,4},{4,8},{8,12},{1,5},{5,9},{9,13},{2,6},{6,10},{10,14},{3,7},{... | collective-permute-start | bytes 1966088 | tf_op jit(solution)/shard_map/ppermute | solution.py:16
  548.2 30.9 %collective-permute-start.23 = (f32[2,640,128]{1,2,0:T(8,128)S(1)}, f32[2,640,128]{1,2,0:T(8,128)S(1)}, u32[]{:S(2)}, u32[]{:S(2)}) collective-permute-start(f32[2,640,128]{1,2,0:T(8,128)S(1)} %get-tuple-element.20), channel_id=1, source_target_pairs={{4,0},{8,4},{12,8},{5,1},{9,5},{13,9},{6,2},{10,6},{14,10},{7,3},{... | collective-permute-start | bytes 1966088 | tf_op jit(solution)/shard_map/ppermute | solution.py:19
  580.1 107.4 %all-reduce.25.cloned.1.call-start = ((), (), s32[]{:S(2)}) async-start(), calls=%async_computation.6 | async-start | bytes 1048576 | tf_op jit(solution)/shard_map/psum | solution.py:155
  614.9 2.6 collective-permute-start.24
  616.2 3.4 collective-permute-start.25
  619.7 12.0 %collective-permute-start.26 = (f32[2,384,128]{1,2,0:T(8,128)S(1)}, f32[2,384,128]{1,2,0:T(8,128)S(1)}, u32[]{:S(2)}, u32[]{:S(2)}) collective-permute-start(f32[2,384,128]{1,2,0:T(8,128)S(1)} %get-tuple-element.59), channel_id=1, source_target_pairs={{0,4},{4,8},{8,12},{1,5},{5,9},{9,13},{2,6},{6,10},{10,14},{3,7},{... | collective-permute-start | bytes 1179656 | tf_op jit(solution)/shard_map/ppermute | solution.py:16
  623.1 19.0 %collective-permute-start.27 = (f32[2,384,128]{1,2,0:T(8,128)S(1)}, f32[2,384,128]{1,2,0:T(8,128)S(1)}, u32[]{:S(2)}, u32[]{:S(2)}) collective-permute-start(f32[2,384,128]{1,2,0:T(8,128)S(1)} %get-tuple-element.60), channel_id=1, source_target_pairs={{4,0},{8,4},{12,8},{5,1},{9,5},{13,9},{6,2},{10,6},{14,10},{7,3},{... | collective-permute-start | bytes 1179656 | tf_op jit(solution)/shard_map/ppermute | solution.py:19
  645.3 1.0 copy-start.30
  646.4 1.6 copy-start.3
  646.4 1.7 copy-start.7
  649.8 138.0 %all-reduce.27.cloned.1.call-start = ((), (), s32[]{:S(2)}) async-start(), calls=%async_computation.7 | async-start | bytes 524288 | tf_op jit(solution)/shard_map/psum | solution.py:158
  688.8 1.0 copy-start.22
  691.5 1.5 copy-start.11
  713.4 2.8 collective-permute-start.28
  714.7 3.8 collective-permute-start.29
  718.6 17.5 %collective-permute-start.30 = (f32[2,640,128]{1,2,0:T(8,128)S(1)}, f32[2,640,128]{1,2,0:T(8,128)S(1)}, u32[]{:S(2)}, u32[]{:S(2)}) collective-permute-start(f32[2,640,128]{1,2,0:T(8,128)S(1)} %get-tuple-element.17), channel_id=1, source_target_pairs={{0,4},{4,8},{8,12},{1,5},{5,9},{9,13},{2,6},{6,10},{10,14},{3,7},{... | collective-permute-start | bytes 1966088 | tf_op jit(solution)/shard_map/ppermute | solution.py:16
  721.9 31.1 %collective-permute-start.31 = (f32[2,640,128]{1,2,0:T(8,128)S(1)}, f32[2,640,128]{1,2,0:T(8,128)S(1)}, u32[]{:S(2)}, u32[]{:S(2)}) collective-permute-start(f32[2,640,128]{1,2,0:T(8,128)S(1)} %get-tuple-element.18), channel_id=1, source_target_pairs={{4,0},{8,4},{12,8},{5,1},{9,5},{13,9},{6,2},{10,6},{14,10},{7,3},{... | collective-permute-start | bytes 1966088 | tf_op jit(solution)/shard_map/ppermute | solution.py:19
  753.2 119.3 %copy-start.17 = (f32[2,128,256]{1,2,0:T(8,128)S(1)}, f32[2,128,256]{1,2,0:T(8,128)}, u32[]{:S(2)}) copy-start(f32[2,128,256]{1,2,0:T(8,128)} %copy-done.16) | copy-start | bytes 786436
  753.2 119.3 %copy-start.26 = (f32[2,128,256]{1,2,0:T(8,128)S(1)}, f32[2,128,256]{1,2,0:T(8,128)}, u32[]{:S(2)}) copy-start(f32[2,128,256]{1,2,0:T(8,128)} %all-reduce.23.cloned.1.call-done) | copy-start | bytes 786436
  (9 other events, 8.6 us)
Sparse Core Ops, SparseCore 0:
  42.6 38.9 all-reduce.12
  148.8 33.5 all-reduce.14
  218.4 37.6 all-reduce.16
  322.5 33.5 all-reduce.18
  476.2 37.3 all-reduce.20
  580.3 33.5 all-reduce.22
  649.9 37.6 all-reduce.24
  754.1 33.5 all-reduce.26
